TPU v7x, 32 devices: a whole 2x2x4 slice. The times are simulated.
32 devices in a mesh: samp: 4 (over z), atom: 8 (over y, x, core).
Axes of the slice: x: 2, y: 2, z: 4, core: 2. Of those that a mesh axis runs over, the one named last changes fastest.
Arguments:
- atom_state: bfloat16 [16, 2560, 128], P('samp', 'atom'), may hold values from -6 to 6, as said below
- atom_token: int32 [2560], P('atom'), may hold values from 0 to 319, never falling along the last dimension, each value on 1 to 24 neighbouring positions
- window_valid: int32 [80], P('atom'), may hold values from 1 to 32
- attend_gain: float32 [128], replicated, may hold values from 0.25 to 1.75
- project_weight: bfloat16 [128, 384], replicated, may hold values from -4 to 4
- output_weight: bfloat16 [128, 128], replicated, may hold values from -1.5 to 1.5
- token_bias: float32 [4], replicated, may hold values from -2 to 2
- transit_gain: float32 [128], replicated, may hold values from 0.25 to 1.75
- transit_weight: bfloat16 [128, 512], replicated, may hold values from -0.5 to 0.5
- return_weight: bfloat16 [256, 128], replicated, may hold values from -0.375 to 0.375
- cotangent: bfloat16 [16, 2560, 128], P('samp', 'atom'), may hold values from -6 to 6
Outputs:
- block_out: bfloat16 [16, 2560, 128], P('samp', 'atom')
- state_grad: bfloat16 [16, 2560, 128], P('samp', 'atom')
- grad_attend_gain: float32 [128], replicated
- grad_project: float32 [128, 384], replicated
- grad_output: float32 [128, 128], replicated
- grad_bias: float32 [4], replicated
- grad_transit_gain: float32 [128], replicated
- grad_transit: float32 [128, 512], replicated
- grad_return: float32 [256, 128], replicated
Inputs may be any that keep to these rules, and one draw needn't show every extreme that they name: atom_state is finite. `atom_token`: tokens are numbered in order along the atoms; a token has 1 to 24 atoms.
All inputs are finite; a program needn't handle non-finite values.
Results may differ from a plain program's by a relative error of at most 0.025.
The roundings to bfloat16 on the way count: a program that leaves them out, or rounds other values in their place, can miss the bound.
Values may be sent and summed in bfloat16 or wider, within the bound.
No kernel may reach another device: no remote copies, remote signals or barrier semaphores. Data moves between devices by JAX's collectives and lax.ppermute only.
A program may use at most 64 MiB of HBM per device.

v0:
```python
import jax
import jax.numpy as jnp
from jax import lax
from jax.sharding import PartitionSpec as P

HEADS = 4
TRANS = 256
QWIN = 32
KWIN = 128
HALO = 48
PRECISE = lax.Precision.HIGHEST
EPSILON = 1e-05
CLIP_NORM = 256.0


def with_halo(value, sides, width):
    for axis, dim in sides:
        size, length = (lax.axis_size(axis), value.shape[dim])
        up = [(i, (i + 1) % size) for i in range(size - 1)]
        down = [(j, i) for i, j in up]
        last = lax.slice_in_dim(value, length - width, length, axis=dim)
        first = lax.slice_in_dim(value, 0, width, axis=dim)
        before = lax.ppermute(last, axis, up)
        after = lax.ppermute(first, axis, down)
        value = jnp.concatenate([before, value, after], axis=dim)
    return value


def passed_along(value, axis, by):
    size = lax.axis_size(axis)
    pairs = [(i, i + by) for i in range(size) if 0 <= i + by < size]
    return lax.ppermute(value, axis, pairs)


def normalize(values, scaling):
    values = values.astype(jnp.float32)
    center = jnp.mean(values, axis=-1, keepdims=True)
    shifted = values - center
    variance = jnp.mean(shifted * shifted, axis=-1, keepdims=True)
    return shifted * lax.rsqrt(variance + EPSILON) * scaling


def token_codes(atom_token, window_valid):
    windows_here = window_valid.shape[0]
    slots = lax.broadcasted_iota(jnp.int32, (windows_here, QWIN), 1)
    inside = (slots < window_valid[:, None]).reshape(-1)
    return jnp.where(inside, atom_token + 1, 0)


def attend(queries, pairs, query_ids, ext_ids, token_bias):
    channels = queries.shape[1]
    window_count = queries.shape[0] // QWIN
    extra_blocks = 2 * HALO // QWIN
    span_blocks = KWIN // QWIN
    head_dim = channels // HEADS
    blocks = pairs.reshape(window_count + extra_blocks, QWIN, 2 * channels)
    gathered = jnp.concatenate(
        [blocks[offset : offset + window_count] for offset in range(span_blocks)], axis=1
    )
    code_blocks = ext_ids.reshape(window_count + extra_blocks, QWIN)
    key_ids = jnp.concatenate(
        [code_blocks[offset : offset + window_count] for offset in range(span_blocks)], axis=1
    )
    query_blocks = queries.reshape(window_count, QWIN, HEADS, head_dim)
    keys_in = gathered[:, :, :channels].reshape(window_count, KWIN, HEADS, head_dim)
    values_in = gathered[:, :, channels:].reshape(window_count, KWIN, HEADS, head_dim)
    scores = jnp.einsum("wqhd,wkhd->whqk", query_blocks, keys_in, precision=PRECISE) / jnp.sqrt(
        float(head_dim)
    )
    query_codes = query_ids.reshape(window_count, QWIN)
    same_token = (query_codes[:, :, None] == key_ids[:, None, :]).astype(jnp.float32)
    scores = scores + token_bias[None, :, None, None] * same_token[:, None, :, :]
    usable_key = (key_ids > 0)[:, None, None, :]
    scores = jnp.where(usable_key, scores, -1e30)
    highest = lax.stop_gradient(jnp.max(scores, axis=-1, keepdims=True))
    weights = jnp.exp(scores - highest)
    weights = weights / jnp.sum(weights, axis=-1, keepdims=True)
    outcome = jnp.einsum("whqk,wkhd->wqhd", weights, values_in, precision=PRECISE)
    return outcome.reshape(window_count * QWIN, channels)


def place_rims(center, from_before, from_after):
    atoms_here = center.shape[1]
    lower = jnp.pad(from_before, ((0, 0), (0, atoms_here - HALO), (0, 0)))
    upper = jnp.pad(from_after, ((0, 0), (atoms_here - HALO, 0), (0, 0)))
    return center + lower + upper


def on_device(
    atom_state,
    atom_token,
    window_valid,
    attend_gain,
    project_weight,
    output_weight,
    token_bias,
    transit_gain,
    transit_weight,
    return_weight,
    cotangent,
):
    channels = atom_state.shape[2]
    atoms_here = atom_state.shape[1]
    query_ids = token_codes(atom_token, window_valid)
    ext_ids = with_halo(query_ids, (("atom", 0),), HALO)
    normed = normalize(atom_state, attend_gain).astype(jnp.bfloat16)
    query_part = project_weight[:, :channels]
    pair_part = project_weight[:, channels:]
    ext_normed = with_halo(normed, (("atom", 1),), HALO)
    queries = jnp.dot(normed, query_part, preferred_element_type=jnp.float32).astype(jnp.bfloat16)
    ext_pairs = jnp.dot(ext_normed, pair_part, preferred_element_type=jnp.float32).astype(
        jnp.bfloat16
    )

    def forward_one(operands):
        query_rows, pair_rows = operands
        return attend(
            query_rows.astype(jnp.float32),
            pair_rows.astype(jnp.float32),
            query_ids,
            ext_ids,
            token_bias,
        )

    attended = lax.map(forward_one, (queries, ext_pairs)).astype(jnp.bfloat16)
    residual = (
        atom_state.astype(jnp.float32)
        + jnp.dot(attended, output_weight, preferred_element_type=jnp.float32)
    ).astype(jnp.bfloat16)
    transit_in = normalize(residual, transit_gain).astype(jnp.bfloat16)
    both_parts = jnp.dot(transit_in, transit_weight, preferred_element_type=jnp.float32)
    gate_part = both_parts[:, :, :TRANS]
    up_part = both_parts[:, :, TRANS:]
    gated = (jax.nn.silu(gate_part) * up_part).astype(jnp.bfloat16)
    block_out = (
        residual.astype(jnp.float32)
        + jnp.dot(gated, return_weight, preferred_element_type=jnp.float32)
    ).astype(jnp.bfloat16)
    grad_return = jnp.einsum("sai,sac->ic", gated, cotangent, preferred_element_type=jnp.float32)
    back_gated = jnp.einsum(
        "sac,ic->sai", cotangent, return_weight, preferred_element_type=jnp.float32
    )
    sigmoid_gate = jax.nn.sigmoid(gate_part)
    back_gate = back_gated * up_part * sigmoid_gate * (1.0 + gate_part * (1.0 - sigmoid_gate))
    back_up = back_gated * gate_part * sigmoid_gate
    back_hidden = jnp.concatenate([back_gate, back_up], axis=-1).astype(jnp.bfloat16)
    grad_transit = jnp.einsum(
        "sac,sae->ce", transit_in, back_hidden, preferred_element_type=jnp.float32
    )
    back_transit = jnp.einsum(
        "sae,ce->sac", back_hidden, transit_weight, preferred_element_type=jnp.float32
    )
    _, pull_second = jax.vjp(normalize, residual.astype(jnp.float32), transit_gain)
    back_res_norm, grad_transit_gain = pull_second(back_transit)
    back_residual = cotangent.astype(jnp.float32) + back_res_norm
    back_res16 = back_residual.astype(jnp.bfloat16)
    grad_output = jnp.einsum(
        "sac,sae->ce", attended, back_res16, preferred_element_type=jnp.float32
    )
    back_attended = jnp.einsum(
        "sae,ce->sac", back_res16, output_weight, preferred_element_type=jnp.float32
    )

    def backward_one(operands):
        query_rows, pair_rows, back_rows = operands

        def local_attend(query_in, pairs_in, bias_in):
            return attend(query_in, pairs_in, query_ids, ext_ids, bias_in)

        _, pull_attend = jax.vjp(
            local_attend, query_rows.astype(jnp.float32), pair_rows.astype(jnp.float32), token_bias
        )
        return pull_attend(back_rows)

    back_queries, back_ext, bias_parts = lax.map(backward_one, (queries, ext_pairs, back_attended))
    grad_bias = jnp.sum(bias_parts, axis=0)
    grad_query = jnp.einsum(
        "sac,sae->ce", normed.astype(jnp.float32), back_queries, precision=PRECISE
    )
    grad_pairs = jnp.einsum(
        "sac,sae->ce", ext_normed.astype(jnp.float32), back_ext, precision=PRECISE
    )
    grad_project = jnp.concatenate([grad_query, grad_pairs], axis=1)
    back_ext_normed = jnp.einsum(
        "sae,ce->sac", back_ext, pair_part.astype(jnp.float32), precision=PRECISE
    )
    from_before = passed_along(
        back_ext_normed[:, HALO + atoms_here :].astype(jnp.bfloat16), "atom", 1
    ).astype(jnp.float32)
    from_after = passed_along(back_ext_normed[:, :HALO].astype(jnp.bfloat16), "atom", -1).astype(
        jnp.float32
    )
    own_rows = back_ext_normed[:, HALO : HALO + atoms_here] + jnp.einsum(
        "sae,ce->sac", back_queries, query_part.astype(jnp.float32), precision=PRECISE
    )
    back_normed = place_rims(own_rows, from_before, from_after)
    _, pull_first = jax.vjp(normalize, atom_state.astype(jnp.float32), attend_gain)
    back_state_norm, grad_attend_gain = pull_first(back_normed)
    state_grad = (back_residual + back_state_norm).astype(jnp.bfloat16)
    gradients = (
        grad_attend_gain,
        grad_project,
        grad_output,
        grad_bias,
        grad_transit_gain,
        grad_transit,
        grad_return,
    )
    totals = lax.psum(
        (
            gradients[0],
            gradients[1],
            gradients[2],
            gradients[3],
            gradients[4],
            gradients[5],
            gradients[6],
        ),
        ("samp", "atom"),
    )
    squares = sum((jnp.sum(member * member) for member in totals))
    factor = CLIP_NORM / jnp.sqrt(squares + CLIP_NORM * CLIP_NORM)
    clipped = tuple((member * factor for member in totals))
    return (
        block_out,
        state_grad,
        clipped[0],
        clipped[1],
        clipped[2],
        clipped[3],
        clipped[4],
        clipped[5],
        clipped[6],
    )


def solution(mesh):
    return jax.shard_map(
        on_device,
        mesh=mesh,
        in_specs=(
            P("samp", "atom", None),
            P("atom"),
            P("atom"),
            P(),
            P(),
            P(),
            P(),
            P(),
            P(),
            P(),
            P("samp", "atom", None),
        ),
        out_specs=(
            P("samp", "atom", None),
            P("samp", "atom", None),
            P(),
            P(),
            P(),
            P(),
            P(),
            P(),
            P(),
        ),
        check_vma=False,
    )
```

profile of v0, /device:TPU:0, one launch (start us, length us, event | category | flops | bytes accessed | tf_op | source)
XLA Modules:
  0.0 380.1 jit_solution(13928921964016010154)
XLA Ops:
  8.9 2.4 collective-permute-start.2
  13.7 1.4 fusion.41
  16.6 5.1 %collective-permute-start = (bf16[4,48,128]{2,1,0:T(8,128)(2,1)S(1)}, bf16[4,48,128]{2,1,0:T(8,128)(2,1)S(1)}, u32[]{:S(2)}, u32[]{:S(2)}) collective-permute-start(bf16[4,48,128]{2,1,0:T(8,128)(2,1)S(1)} %get-tuple-element.304), channel_id=1, source_target_pairs={{0,1},{1,2},{2,3},{3,4},{4,5},{5,6},{6,7},{8,9},{9,10},{10,11},{11... | collective-permute-start | bytes 147464 | tf_op jit(solution)/shard_map/ppermute | solution.py:23
  27.4 67.5 %while.30 = (s32[]{:T(128)}, bf16[4,320,128]{2,1,0:T(8,128)(2,1)}, bf16[4,416,256]{2,1,0:T(8,128)(2,1)}, s32[10,1,1,128]{3,0,2,1:T(8,128)S(1)}, bf16[4,320,128]{...) while((s32[]{:T(128)}, bf16[4,320,128]{2,1,0:T(8,128)(2,1)}, ...), condition=%wide.region_5.6_spmd.clone, body=%wide.region_2.5_spmd.sunk.clone | while | flops 128473856 | bytes 16410097 | solution.py:125
  33.0 2.4 copy.101
  35.5 1.5 copy.102
  36.9 2.8 pad_maximum_fusion.13
  49.9 2.4 copy.101
  52.3 1.5 copy.102
  53.8 2.8 pad_maximum_fusion.13
  66.7 2.4 copy.101
  69.2 1.5 copy.102
  70.7 2.8 pad_maximum_fusion.13
  83.6 2.4 copy.101
  86.0 1.5 copy.102
  87.5 2.8 pad_maximum_fusion.13
  94.8 1.5 fusion.83
  100.8 1.6 convolution_bitcast_fusion.2
  106.7 102.9 %while.31 = (s32[]{:T(128)}, f32[4,320,128]{2,1,0:T(8,128)}, f32[4,416,256]{2,1,0:T(8,128)}, f32[4,4]{1,0:T(4,128)S(1)}, s32[10,1,1,128]{3,0,2,1:T(8,128)S(1)}, ...) while((s32[]{:T(128)}, f32[4,320,128]{2,1,0:T(8,128)}, ...), condition=%wide.region_15.16_spmd.clone, body=%wide.region_10.15_spmd.sunk.clone | while | flops 319997184 | bytes 31044328 | solution.py:175
  114.3 2.4 copy.108
  116.7 2.4 copy.109
  119.2 2.8 pad_maximum_fusion.14
  124.5 1.6 fusion.172
  139.9 2.4 copy.108
  142.4 2.4 copy.109
  144.8 2.8 pad_maximum_fusion.14
  150.1 1.6 fusion.172
  165.6 2.4 copy.108
  168.1 2.4 copy.109
  170.5 2.8 pad_maximum_fusion.14
  175.8 1.6 fusion.172
  191.3 2.4 copy.108
  193.7 2.4 copy.109
  196.2 2.8 pad_maximum_fusion.14
  201.5 1.6 fusion.172
  209.6 2.5 fusion.84
  212.7 4.7 %collective-permute-start.4 = (bf16[4,48,128]{2,1,0:T(8,128)(2,1)S(1)}, bf16[4,48,128]{2,1,0:T(8,128)(2,1)S(1)}, u32[]{:S(2)}, u32[]{:S(2)}) collective-permute-start(bf16[4,48,128]{2,1,0:T(8,128)(2,1)S(1)} %get-tuple-element.302), channel_id=1, source_target_pairs={{0,1},{1,2},{2,3},{3,4},{4,5},{5,6},{6,7},{8,9},{9,10},{10,11},{11... | collective-permute-start | bytes 147464 | tf_op jit(solution)/shard_map/ppermute | solution.py:32
  217.4 1.4 collective-permute-start.5
  221.2 1.8 fusion.42
  223.9 44.4 %all-reduce.8 = (f32[128]{0:T(128)S(1)}, f32[4]{0:T(128)S(1)}, f32[128]{0:T(128)S(1)}) all-reduce(f32[128]{0:T(128)S(1)} %get-tuple-element.226, f32[4]{0:T(128)S(1)} %reduce_sum.232, f32[128]{0:T(128)S(1)} %copy-done.29), channel_id=1, replica_groups=mesh['samp'=4,'atom'=8] {'samp','atom'}, use_global_device_ids=true, to_apply=%region_19.20 | all-reduce | flops 260 | bytes 2080 | tf_op jit(solution)/shard_map/psum | solution.py:209
  270.2 1.7 add_convert_fusion
  271.9 84.5 %all-reduce.12.cloned.1.call-done = (f32[128,384]{1,0:T(8,128)}, f32[128,128]{1,0:T(8,128)}, f32[128,512]{1,0:T(8,128)}, f32[256,128]{1,0:T(8,128)}) async-done(((f32[128,384]{1,0:T(8,128)}, f32[128,128]{1,0:T(8,128)}, f32[128,512]{1,0:T(8,128)}, f32[256,128]{1,0:T(8,128)}), (f32[128,384]{1,0:T(8,128)}, f32[128,128]{1,0:T(8,128)}, f32[128,512]{1,0:T(8,128)}, ...) | async-done | bytes 655376 | tf_op jit(solution)/shard_map/psum | solution.py:209
  356.4 1.6 multiply_reduce_fusion.7
  358.0 1.6 multiply_reduce_fusion.5
  359.6 1.5 multiply_reduce_fusion.8
  361.0 1.6 multiply_reduce_fusion.6
  367.7 1.6 broadcast_multiply_fusion.2
  369.2 1.7 broadcast_multiply_fusion
  (325 shorter events, 133.8 us)
Async XLA Ops:
  7.2 89.7 %copy-start = (bf16[128,512]{1,0:T(8,128)(2,1)S(1)}, bf16[128,512]{1,0:T(8,128)(2,1)}, u32[]{:S(2)}) copy-start(bf16[128,512]{1,0:T(8,128)(2,1)} %param.23) | copy-start | bytes 393220
  7.2 16.6 %copy-start.15 = (bf16[128,384]{1,0:T(8,128)(2,1)S(1)}, bf16[128,384]{1,0:T(8,128)(2,1)}, u32[]{:S(2)}) copy-start(bf16[128,384]{1,0:T(8,128)(2,1)} %param.19) | copy-start | bytes 294916
  7.2 349.2 %all-reduce.12.cloned.1.call-start = ((), (), s32[]{:S(2)}) async-start(), calls=%async_computation | async-start | bytes 1310720 | tf_op jit(solution)/shard_map/psum | solution.py:209
  8.9 15.9 %collective-permute-start.2 = (s32[48]{0:T(128)S(1)}, s32[48]{0:T(128)S(1)}, u32[]{:S(2)}, u32[]{:S(2)}) collective-permute-start(s32[48]{0:T(128)S(1)} %get-tuple-element.310), channel_id=1, source_target_pairs={{0,1},{1,2},{2,3},{3,4},{4,5},{5,6},{6,7},{8,9},{9,10},{10,11},{11... | collective-permute-start | bytes 584 | tf_op jit(solution)/shard_map/ppermute | solution.py:23
  11.3 13.5 %collective-permute-start.3 = (s32[48]{0:T(128)S(1)}, s32[48]{0:T(128)S(1)}, u32[]{:S(2)}, u32[]{:S(2)}) collective-permute-start(s32[48]{0:T(128)S(1)} %get-tuple-element.311), channel_id=1, source_target_pairs={{1,0},{2,1},{3,2},{4,3},{5,4},{6,5},{7,6},{9,8},{10,9},{11,10},{12... | collective-permute-start | bytes 584 | tf_op jit(solution)/shard_map/ppermute | solution.py:24
  16.6 10.8 %copy-start.5 = (bf16[4,320,128]{2,1,0:T(8,128)(2,1)}, bf16[4,320,128]{2,1,0:T(8,128)(2,1)S(1)}, u32[]{:S(2)}) copy-start(bf16[4,320,128]{2,1,0:T(8,128)(2,1)S(1)} %fusion.39) | copy-start | bytes 983044
  16.6 9.1 %collective-permute-start = (bf16[4,48,128]{2,1,0:T(8,128)(2,1)S(1)}, bf16[4,48,128]{2,1,0:T(8,128)(2,1)S(1)}, u32[]{:S(2)}, u32[]{:S(2)}) collective-permute-start(bf16[4,48,128]{2,1,0:T(8,128)(2,1)S(1)} %get-tuple-element.304), channel_id=1, source_target_pairs={{0,1},{1,2},{2,3},{3,4},{4,5},{5,6},{6,7},{8,9},{9,10},{10,11},{11... | collective-permute-start | bytes 147464 | tf_op jit(solution)/shard_map/ppermute | solution.py:23
  21.7 4.4 %collective-permute-start.1 = (bf16[4,48,128]{2,1,0:T(8,128)(2,1)S(1)}, bf16[4,48,128]{2,1,0:T(8,128)(2,1)S(1)}, u32[]{:S(2)}, u32[]{:S(2)}) collective-permute-start(bf16[4,48,128]{2,1,0:T(8,128)(2,1)S(1)} %get-tuple-element.305), channel_id=1, source_target_pairs={{1,0},{2,1},{3,2},{4,3},{5,4},{6,5},{7,6},{9,8},{10,9},{11,10},{12... | collective-permute-start | bytes 147464 | tf_op jit(solution)/shard_map/ppermute | solution.py:24
  25.7 1.6 copy-start.20
  26.1 1.3 copy-start.22
  39.7 0.9 copy-start.2
  39.7 0.9 copy-start.18
  56.6 0.9 copy-start.2
  56.6 0.9 copy-start.18
  73.4 0.9 copy-start.2
  73.5 0.9 copy-start.18
  90.3 0.9 copy-start.2
  90.3 0.9 copy-start.18
  94.8 2.0 copy-start.25
  96.9 1.0 copy-start.9
  96.9 1.0 copy-start.17
  103.5 1.1 copy-start.11
  104.4 2.3 copy-start.7
  104.4 1.2 copy-start.16
  104.4 2.3 copy-start.19
  104.4 2.3 copy-start.26
  122.1 1.3 copy-start.1
  147.7 1.3 copy-start.1
  173.4 1.3 copy-start.1
  199.1 1.3 copy-start.1
  209.6 2.5 copy-start.27
  209.6 2.5 copy-start.6
  209.6 2.5 copy-start.12
  209.6 9.2 %copy-start.4 = (f32[4,416,256]{2,1,0:T(8,128)S(1)}, f32[4,416,256]{2,1,0:T(8,128)}, u32[]{:S(2)}) copy-start(f32[4,416,256]{2,1,0:T(8,128)} %get-tuple-element.221) | copy-start | bytes 5111812
  209.6 9.3 %copy-start.21 = (bf16[4,48,128]{2,1,0:T(8,128)(2,1)S(1)}, bf16[4,48,128]{2,1,0:T(8,128)(2,1)}, u32[]{:S(2)}) copy-start(bf16[4,48,128]{2,1,0:T(8,128)(2,1)} %copy-done.20) | copy-start | bytes 147460
  209.6 9.3 %copy-start.23 = (bf16[4,48,128]{2,1,0:T(8,128)(2,1)S(1)}, bf16[4,48,128]{2,1,0:T(8,128)(2,1)}, u32[]{:S(2)}) copy-start(bf16[4,48,128]{2,1,0:T(8,128)(2,1)} %copy-done.22) | copy-start | bytes 147460
  212.7 7.8 %collective-permute-start.4 = (bf16[4,48,128]{2,1,0:T(8,128)(2,1)S(1)}, bf16[4,48,128]{2,1,0:T(8,128)(2,1)S(1)}, u32[]{:S(2)}, u32[]{:S(2)}) collective-permute-start(bf16[4,48,128]{2,1,0:T(8,128)(2,1)S(1)} %get-tuple-element.302), channel_id=1, source_target_pairs={{0,1},{1,2},{2,3},{3,4},{4,5},{5,6},{6,7},{8,9},{9,10},{10,11},{11... | collective-permute-start | bytes 147464 | tf_op jit(solution)/shard_map/ppermute | solution.py:32
  217.4 3.1 copy-start.28
  217.4 3.8 copy-start.3
  217.4 3.8 copy-start.24
  217.4 3.7 collective-permute-start.5
  221.2 2.8 copy-start.29
  221.2 49.1 %copy-start.8 = (f32[4,320,128]{2,1,0:T(8,128)S(1)}, f32[4,320,128]{2,1,0:T(8,128)}, u32[]{:S(2)}) copy-start(f32[4,320,128]{2,1,0:T(8,128)} %copy-done.7) | copy-start | bytes 1966084
  221.2 49.1 %copy-start.10 = (bf16[4,320,128]{2,1,0:T(8,128)(2,1)S(1)}, bf16[4,320,128]{2,1,0:T(8,128)(2,1)}, u32[]{:S(2)}) copy-start(bf16[4,320,128]{2,1,0:T(8,128)(2,1)} %param.25) | copy-start | bytes 983044
  356.4 15.1 %copy-start.14 = (f32[128,128]{1,0:T(8,128)S(1)}, f32[128,128]{1,0:T(8,128)}, u32[]{:S(2)}) copy-start(f32[128,128]{1,0:T(8,128)} %get-tuple-element.270) | copy-start | bytes 196612
  356.4 15.7 %copy-start.13 = (f32[128,384]{1,0:T(8,128)S(1)}, f32[128,384]{1,0:T(8,128)}, u32[]{:S(2)}) copy-start(f32[128,384]{1,0:T(8,128)} %get-tuple-element.269) | copy-start | bytes 589828
Sparse Core Ops, SparseCore 0:
  220.6 135.7 all-reduce.11
where the time goes:
time: 383 us; the launch traced here: 380 us
  local copies, waits for them, and re-layouts  96.1 us (25%)
  waiting for transfers between devices  85.5 us (22%)
  other arithmetic  71.7 us (19%)
  matrix products  46 us (12%)
  blocking collectives  44.4 us (12%)
  between operations  19 us (5%)
  starting transfers between devices  16.2 us (4%)
    psum x1, waiting for transfers between devices, on_device(): lax.psum((gradients[0], gradients[1], gradients[2], gradients[3], gradien...  84.5 us
    slice x40, local copies, waits for them, and re-layouts, attend(): blocks[offset:offset + window_count]  57.2 us
    psum x1, blocking collectives, on_device(): lax.psum((gradients[0], gradients[1], gradients[2], gradients[3], gradien...  44.4 us
    concatenate x8, other arithmetic, attend(): jnp.concatenate([blocks[offset:offset + window_count] for offset in range...  22.3 us
    dot_general x12, matrix products, attend(): jnp.einsum('whqk,wkhd->wqhd', weights, values_in, precision=PRECISE)  16.2 us
    dot_general x16, matrix products, attend(): jnp.einsum('wqhd,wkhd->whqk', query_blocks, keys_in, precision=PRECISE)  12.1 us
    reduce_sum x7, other arithmetic, on_device(): squares = sum((jnp.sum(member * member) for member in totals))  8.12 us
  transfers between devices with their start and end apart: 7, of which 3 were waited for; matrix products, arithmetic and copies ran while one was open for 4% of the time, Pallas kernels for 0%

commit v1 on v0

--- a/solution.py
+++ b/solution.py
@@ -207,16 +207,19 @@
         grad_return,
     )
     totals = lax.psum(
-        (
-            gradients[0],
-            gradients[1],
-            gradients[2],
-            gradients[3],
-            gradients[4],
-            gradients[5],
-            gradients[6],
+        lax.psum(
+            (
+                gradients[0],
+                gradients[1],
+                gradients[2],
+                gradients[3],
+                gradients[4],
+                gradients[5],
+                gradients[6],
+            ),
+            "samp",
         ),
-        ("samp", "atom"),
+        "atom",
     )
     squares = sum((jnp.sum(member * member) for member in totals))
     factor = CLIP_NORM / jnp.sqrt(squares + CLIP_NORM * CLIP_NORM)

time: 383 us -> 350 us (0.914)
  blocking collectives: 44.4 us -> 26.5 us
  waiting for transfers between devices: 85.5 us -> 73 us
    psum x1, waiting for transfers between devices: 84.5 us -> 15.4 us  [on_device(): lax.psum((gradients[0], gradients[1], gradients[2], gradients[3], gradien...]
    psum x0 -> x1, waiting for transfers between devices: none -> 56.6 us  [on_device(): lax.psum(lax.psum((gradients[0], gradients[1], gradients[2], gradients[3]...]
    psum x1, blocking collectives: 44.4 us -> 12.1 us  [on_device(): lax.psum((gradients[0], gradients[1], gradients[2], gradients[3], gradien...]
    psum x0 -> x1, blocking collectives: none -> 14.4 us  [on_device(): lax.psum(lax.psum((gradients[0], gradients[1], gradients[2], gradients[3]...]
  transfers between devices with their start and end apart: 7 -> 8, of which waited for: 3 -> 4; matrix products, arithmetic and copies ran while one was open for 4% -> 4% of each run, Pallas kernels for 0% -> 0%
where the time goes in v1:
time: 350 us; the launch traced here: 348 us
  local copies, waits for them, and re-layouts  96.1 us (27%)
  waiting for transfers between devices  73 us (21%)
  other arithmetic  71.7 us (20%)
  matrix products  44.4 us (13%)
  blocking collectives  26.5 us (8%)
  between operations  19 us (5%)
  starting transfers between devices  16.3 us (5%)
    slice x40, local copies, waits for them, and re-layouts, attend(): blocks[offset:offset + window_count]  57.2 us
    psum x1, waiting for transfers between devices, on_device(): lax.psum(lax.psum((gradients[0], gradients[1], gradients[2], gradients[3]...  56.6 us
    concatenate x8, other arithmetic, attend(): jnp.concatenate([blocks[offset:offset + window_count] for offset in range...  22.3 us
    dot_general x12, matrix products, attend(): jnp.einsum('whqk,wkhd->wqhd', weights, values_in, precision=PRECISE)  16.2 us
    psum x1, waiting for transfers between devices, on_device(): lax.psum((gradients[0], gradients[1], gradients[2], gradients[3], gradien...  15.4 us
    psum x1, blocking collectives, on_device(): lax.psum(lax.psum((gradients[0], gradients[1], gradients[2], gradients[3]...  14.4 us
    dot_general x16, matrix products, attend(): jnp.einsum('wqhd,wkhd->whqk', query_blocks, keys_in, precision=PRECISE)  12.2 us
    psum x1, blocking collectives, on_device(): lax.psum((gradients[0], gradients[1], gradients[2], gradients[3], gradien...  12.1 us
  transfers between devices with their start and end apart: 8, of which 4 were waited for; matrix products, arithmetic and copies ran while one was open for 4% of the time, Pallas kernels for 0%

profile of v1, /device:TPU:0, one launch (start us, length us, event | category | flops | bytes accessed | tf_op | source)
XLA Modules:
  0.0 348.1 jit_solution(935465914198966)
XLA Ops:
  8.9 2.4 collective-permute-start.2
  13.7 1.4 fusion.41
  16.6 5.1 %collective-permute-start = (bf16[4,48,128]{2,1,0:T(8,128)(2,1)S(1)}, bf16[4,48,128]{2,1,0:T(8,128)(2,1)S(1)}, u32[]{:S(2)}, u32[]{:S(2)}) collective-permute-start(bf16[4,48,128]{2,1,0:T(8,128)(2,1)S(1)} %get-tuple-element.311), channel_id=1, source_target_pairs={{0,1},{1,2},{2,3},{3,4},{4,5},{5,6},{6,7},{8,9},{9,10},{10,11},{11... | collective-permute-start | bytes 147464 | tf_op jit(solution)/shard_map/ppermute | solution.py:23
  27.4 67.5 %while.30 = (s32[]{:T(128)}, bf16[4,320,128]{2,1,0:T(8,128)(2,1)}, bf16[4,416,256]{2,1,0:T(8,128)(2,1)}, s32[10,1,1,128]{3,0,2,1:T(8,128)S(1)}, bf16[4,320,128]{...) while((s32[]{:T(128)}, bf16[4,320,128]{2,1,0:T(8,128)(2,1)}, ...), condition=%wide.region_5.6_spmd.clone, body=%wide.region_2.5_spmd.sunk.clone | while | flops 128473856 | bytes 16410097 | solution.py:125
  33.0 2.4 copy.101
  35.5 1.5 copy.102
  36.9 2.8 pad_maximum_fusion.13
  49.9 2.4 copy.101
  52.3 1.5 copy.102
  53.8 2.8 pad_maximum_fusion.13
  66.7 2.4 copy.101
  69.2 1.5 copy.102
  70.7 2.8 pad_maximum_fusion.13
  83.6 2.4 copy.101
  86.0 1.5 copy.102
  87.5 2.8 pad_maximum_fusion.13
  94.8 1.5 fusion.83
  100.8 1.6 convolution_bitcast_fusion.2
  106.3 102.9 %while.31 = (s32[]{:T(128)}, f32[4,320,128]{2,1,0:T(8,128)}, f32[4,416,256]{2,1,0:T(8,128)}, f32[4,4]{1,0:T(4,128)S(1)}, s32[10,1,1,128]{3,0,2,1:T(8,128)S(1)}, ...) while((s32[]{:T(128)}, f32[4,320,128]{2,1,0:T(8,128)}, ...), condition=%wide.region_15.16_spmd.clone, body=%wide.region_10.15_spmd.sunk.clone | while | flops 319997184 | bytes 31044328 | solution.py:175
  113.9 2.4 copy.108
  116.3 2.4 copy.109
  118.8 2.8 pad_maximum_fusion.14
  124.1 1.6 fusion.172
  139.6 2.4 copy.108
  142.0 2.4 copy.109
  144.4 2.8 pad_maximum_fusion.14
  149.7 1.6 fusion.172
  165.2 2.4 copy.108
  167.7 2.4 copy.109
  170.1 2.8 pad_maximum_fusion.14
  175.4 1.6 fusion.172
  190.9 2.4 copy.108
  193.4 2.4 copy.109
  195.8 2.8 pad_maximum_fusion.14
  201.1 1.6 fusion.172
  209.2 2.5 fusion.84
  212.3 4.7 %collective-permute-start.4 = (bf16[4,48,128]{2,1,0:T(8,128)(2,1)S(1)}, bf16[4,48,128]{2,1,0:T(8,128)(2,1)S(1)}, u32[]{:S(2)}, u32[]{:S(2)}) collective-permute-start(bf16[4,48,128]{2,1,0:T(8,128)(2,1)S(1)} %get-tuple-element.309), channel_id=1, source_target_pairs={{0,1},{1,2},{2,3},{3,4},{4,5},{5,6},{6,7},{8,9},{9,10},{10,11},{11... | collective-permute-start | bytes 147464 | tf_op jit(solution)/shard_map/ppermute | solution.py:32
  222.3 12.1 %all-reduce.10 = (f32[128]{0:T(128)S(1)}, f32[4]{0:T(128)S(1)}, f32[128]{0:T(128)S(1)}) all-reduce(f32[128]{0:T(128)S(1)} %get-tuple-element.226, f32[4]{0:T(128)S(1)} %reduce_sum.232, f32[128]{0:T(128)S(1)} %get-tuple-element.224), channel_id=1, replica_groups=mesh['samp'=4,'atom'=8] {'samp'}, use_global_device_ids=true, to_apply=%region_19.20 | all-reduce | flops 260 | bytes 2080 | tf_op jit(solution)/shard_map/psum | solution.py:210
  234.5 14.4 %all-reduce.8 = (f32[128]{0:T(128)S(1)}, f32[4]{0:T(128)S(1)}, f32[128]{0:T(128)S(1)}) all-reduce(f32[128]{0:T(128)S(1)} %get-tuple-element.273, f32[4]{0:T(128)S(1)} %get-tuple-element.274, f32[128]{0:T(128)S(1)} %get-tuple-element.275), channel_id=1, replica_groups=mesh['samp'=4,'atom'=8] {'atom'}, use_global_device_ids=true, to_apply=%region_20.21 | all-reduce | flops 260 | bytes 2080 | tf_op jit(solution)/shard_map/psum | solution.py:209
  250.1 15.4 %all-reduce.17.cloned.1.call-done = (f32[128,384]{1,0:T(8,128)}, f32[128,128]{1,0:T(8,128)}, f32[128,512]{1,0:T(8,128)}, f32[256,128]{1,0:T(8,128)}) async-done(((f32[128,384]{1,0:T(8,128)}, f32[128,128]{1,0:T(8,128)}, f32[128,512]{1,0:T(8,128)}, f32[256,128]{1,0:T(8,128)}), (f32[128,384]{1,0:T(8,128)}, f32[128,128]{1,0:T(8,128)}, f32[128,512]{1,0:T(8,128)}, ...) | async-done | bytes 655376 | tf_op jit(solution)/shard_map/psum | solution.py:210
  266.2 1.7 add_convert_fusion
  267.8 56.6 %all-reduce.15.cloned.1.call-done = (f32[128,384]{1,0:T(8,128)}, f32[128,128]{1,0:T(8,128)}, f32[128,512]{1,0:T(8,128)}, f32[256,128]{1,0:T(8,128)}) async-done(((f32[128,384]{1,0:T(8,128)}, f32[128,128]{1,0:T(8,128)}, f32[128,512]{1,0:T(8,128)}, f32[256,128]{1,0:T(8,128)}), (f32[128,384]{1,0:T(8,128)}, f32[128,128]{1,0:T(8,128)}, f32[128,512]{1,0:T(8,128)}, ...) | async-done | bytes 655376 | tf_op jit(solution)/shard_map/psum | solution.py:209
  324.4 1.6 multiply_reduce_fusion.7
  326.0 1.6 multiply_reduce_fusion.5
  327.6 1.5 multiply_reduce_fusion.8
  329.1 1.6 multiply_reduce_fusion.6
  335.7 1.6 broadcast_multiply_fusion.2
  337.3 1.7 broadcast_multiply_fusion
  (323 shorter events, 135.5 us)
Async XLA Ops:
  7.2 89.7 %copy-start = (bf16[128,512]{1,0:T(8,128)(2,1)S(1)}, bf16[128,512]{1,0:T(8,128)(2,1)}, u32[]{:S(2)}) copy-start(bf16[128,512]{1,0:T(8,128)(2,1)} %param.23) | copy-start | bytes 393220
  7.2 16.6 %copy-start.15 = (bf16[128,384]{1,0:T(8,128)(2,1)S(1)}, bf16[128,384]{1,0:T(8,128)(2,1)}, u32[]{:S(2)}) copy-start(bf16[128,384]{1,0:T(8,128)(2,1)} %param.19) | copy-start | bytes 294916
  7.2 258.3 %all-reduce.17.cloned.1.call-start = ((), (), s32[]{:S(2)}) async-start(), calls=%async_computation.1 | async-start | bytes 1310720 | tf_op jit(solution)/shard_map/psum | solution.py:210
  8.9 15.9 %collective-permute-start.2 = (s32[48]{0:T(128)S(1)}, s32[48]{0:T(128)S(1)}, u32[]{:S(2)}, u32[]{:S(2)}) collective-permute-start(s32[48]{0:T(128)S(1)} %get-tuple-element.317), channel_id=1, source_target_pairs={{0,1},{1,2},{2,3},{3,4},{4,5},{5,6},{6,7},{8,9},{9,10},{10,11},{11... | collective-permute-start | bytes 584 | tf_op jit(solution)/shard_map/ppermute | solution.py:23
  11.3 13.5 %collective-permute-start.3 = (s32[48]{0:T(128)S(1)}, s32[48]{0:T(128)S(1)}, u32[]{:S(2)}, u32[]{:S(2)}) collective-permute-start(s32[48]{0:T(128)S(1)} %get-tuple-element.318), channel_id=1, source_target_pairs={{1,0},{2,1},{3,2},{4,3},{5,4},{6,5},{7,6},{9,8},{10,9},{11,10},{12... | collective-permute-start | bytes 584 | tf_op jit(solution)/shard_map/ppermute | solution.py:24
  16.6 10.8 %copy-start.5 = (bf16[4,320,128]{2,1,0:T(8,128)(2,1)}, bf16[4,320,128]{2,1,0:T(8,128)(2,1)S(1)}, u32[]{:S(2)}) copy-start(bf16[4,320,128]{2,1,0:T(8,128)(2,1)S(1)} %fusion.39) | copy-start | bytes 983044
  16.6 9.1 %collective-permute-start = (bf16[4,48,128]{2,1,0:T(8,128)(2,1)S(1)}, bf16[4,48,128]{2,1,0:T(8,128)(2,1)S(1)}, u32[]{:S(2)}, u32[]{:S(2)}) collective-permute-start(bf16[4,48,128]{2,1,0:T(8,128)(2,1)S(1)} %get-tuple-element.311), channel_id=1, source_target_pairs={{0,1},{1,2},{2,3},{3,4},{4,5},{5,6},{6,7},{8,9},{9,10},{10,11},{11... | collective-permute-start | bytes 147464 | tf_op jit(solution)/shard_map/ppermute | solution.py:23
  21.7 4.4 %collective-permute-start.1 = (bf16[4,48,128]{2,1,0:T(8,128)(2,1)S(1)}, bf16[4,48,128]{2,1,0:T(8,128)(2,1)S(1)}, u32[]{:S(2)}, u32[]{:S(2)}) collective-permute-start(bf16[4,48,128]{2,1,0:T(8,128)(2,1)S(1)} %get-tuple-element.312), channel_id=1, source_target_pairs={{1,0},{2,1},{3,2},{4,3},{5,4},{6,5},{7,6},{9,8},{10,9},{11,10},{12... | collective-permute-start | bytes 147464 | tf_op jit(solution)/shard_map/ppermute | solution.py:24
  25.7 1.6 copy-start.20
  26.1 1.3 copy-start.22
  39.7 0.9 copy-start.2
  39.7 0.9 copy-start.18
  56.6 0.9 copy-start.2
  56.6 0.9 copy-start.18
  73.4 0.9 copy-start.2
  73.5 0.9 copy-start.18
  90.3 0.9 copy-start.2
  90.3 0.9 copy-start.18
  94.8 2.0 copy-start.25
  96.9 1.0 copy-start.9
  96.9 1.0 copy-start.17
  103.1 1.1 copy-start.11
  104.0 2.3 copy-start.7
  104.0 1.2 copy-start.16
  104.0 2.3 copy-start.19
  104.0 2.3 copy-start.26
  121.7 1.3 copy-start.1
  147.3 1.3 copy-start.1
  173.0 1.3 copy-start.1
  198.7 1.3 copy-start.1
  209.2 2.5 copy-start.6
  209.2 2.5 copy-start.12
  209.2 9.2 %copy-start.4 = (f32[4,416,256]{2,1,0:T(8,128)S(1)}, f32[4,416,256]{2,1,0:T(8,128)}, u32[]{:S(2)}) copy-start(f32[4,416,256]{2,1,0:T(8,128)} %get-tuple-element.221) | copy-start | bytes 5111812
  209.2 9.2 %copy-start.21 = (bf16[4,48,128]{2,1,0:T(8,128)(2,1)S(1)}, bf16[4,48,128]{2,1,0:T(8,128)(2,1)}, u32[]{:S(2)}) copy-start(bf16[4,48,128]{2,1,0:T(8,128)(2,1)} %copy-done.20) | copy-start | bytes 147460
  209.2 9.2 %copy-start.23 = (bf16[4,48,128]{2,1,0:T(8,128)(2,1)S(1)}, bf16[4,48,128]{2,1,0:T(8,128)(2,1)}, u32[]{:S(2)}) copy-start(bf16[4,48,128]{2,1,0:T(8,128)(2,1)} %copy-done.22) | copy-start | bytes 147460
  212.3 7.8 %collective-permute-start.4 = (bf16[4,48,128]{2,1,0:T(8,128)(2,1)S(1)}, bf16[4,48,128]{2,1,0:T(8,128)(2,1)S(1)}, u32[]{:S(2)}, u32[]{:S(2)}) collective-permute-start(bf16[4,48,128]{2,1,0:T(8,128)(2,1)S(1)} %get-tuple-element.309), channel_id=1, source_target_pairs={{0,1},{1,2},{2,3},{3,4},{4,5},{5,6},{6,7},{8,9},{9,10},{10,11},{11... | collective-permute-start | bytes 147464 | tf_op jit(solution)/shard_map/ppermute | solution.py:32
  217.0 3.8 %copy-start.3 = (bf16[4,320,128]{2,1,0:T(8,128)(2,1)S(1)}, bf16[4,320,128]{2,1,0:T(8,128)(2,1)}, u32[]{:S(2)}) copy-start(bf16[4,320,128]{2,1,0:T(8,128)(2,1)} %param.15) | copy-start | bytes 983044
  217.0 3.8 %copy-start.24 = (f32[128]{0:T(128)S(1)}, f32[128]{0:T(128)}, u32[]{:S(2)}) copy-start(f32[128]{0:T(128)} %param.18) | copy-start | bytes 1540
  217.0 3.7 %collective-permute-start.5 = (bf16[4,48,128]{2,1,0:T(8,128)(2,1)S(1)}, bf16[4,48,128]{2,1,0:T(8,128)(2,1)S(1)}, u32[]{:S(2)}, u32[]{:S(2)}) collective-permute-start(bf16[4,48,128]{2,1,0:T(8,128)(2,1)S(1)} %get-tuple-element.310), channel_id=1, source_target_pairs={{1,0},{2,1},{3,2},{4,3},{5,4},{6,5},{7,6},{9,8},{10,9},{11,10},{12... | collective-permute-start | bytes 147464 | tf_op jit(solution)/shard_map/ppermute | solution.py:32
  220.1 104.3 %all-reduce.15.cloned.1.call-start = ((), (), s32[]{:S(2)}) async-start(), calls=%async_computation | async-start | bytes 1310720 | tf_op jit(solution)/shard_map/psum | solution.py:209
  221.4 44.8 %copy-start.8 = (f32[4,320,128]{2,1,0:T(8,128)S(1)}, f32[4,320,128]{2,1,0:T(8,128)}, u32[]{:S(2)}) copy-start(f32[4,320,128]{2,1,0:T(8,128)} %copy-done.7) | copy-start | bytes 1966084
  221.4 44.8 %copy-start.10 = (bf16[4,320,128]{2,1,0:T(8,128)(2,1)S(1)}, bf16[4,320,128]{2,1,0:T(8,128)(2,1)}, u32[]{:S(2)}) copy-start(bf16[4,320,128]{2,1,0:T(8,128)(2,1)} %param.25) | copy-start | bytes 983044
  324.4 15.1 %copy-start.14 = (f32[128,128]{1,0:T(8,128)S(1)}, f32[128,128]{1,0:T(8,128)}, u32[]{:S(2)}) copy-start(f32[128,128]{1,0:T(8,128)} %get-tuple-element.270) | copy-start | bytes 196612
  324.4 15.7 %copy-start.13 = (f32[128,384]{1,0:T(8,128)S(1)}, f32[128,384]{1,0:T(8,128)}, u32[]{:S(2)}) copy-start(f32[128,384]{1,0:T(8,128)} %get-tuple-element.269) | copy-start | bytes 589828
Sparse Core Ops, SparseCore 0:
  220.2 45.3 all-reduce.16
  269.0 55.3 all-reduce.14
